TPU v7x, 256 devices: a whole 4x4x8 slice. The times are simulated.
256 devices in a mesh: grp: 8 (over y_hi, x), frag: 32 (over y_lo, z, core).
Axes of the slice: x: 4, y: 4 (y_hi: 2, y_lo: 2; y = y_hi * 2 + y_lo), z: 8, core: 2. Of those that a mesh axis runs over, the one named last changes fastest.
Arguments:
- density: bfloat16 [256, 9216], P('frag'), may hold values from -0.1 to 1, as said below
- fock_blocks: bfloat16 [256, 9216], P('frag'), may hold values from -8 to 8, as said below
- coupling: bfloat16 [1024, 9216], P(('grp', 'frag')), may hold values from -1.796875 to 1.796875
- dimer_pairs: int32 [1024, 2], P(('grp', 'frag')), may hold values from 0 to 255, as said below
- atom_counts: int32 [256], P('frag'), may hold values from 8 to 16
- nuclear_charge: float32 [4096], P('frag'), may hold values from 4 to 12
- coords: float32 [3, 4096], P(None, 'frag'), may hold values from -120 to 120
Outputs:
- density_correction: float32 [256, 9216], P('frag')
- dimer_energy: float32 [1024], P(('grp', 'frag'))
- total_energy: float32 [], replicated
Inputs may be any that keep to these rules, and one draw needn't show every extreme that they name: `dimer_pairs`: dimer d has fragments I < J; I // 8 == (d // 4) % 32, and J // 8 lies between I // 8 and I // 8 + 3. `density`: each row is a symmetric matrix. `fock_blocks`: each row is a symmetric matrix.
All inputs are finite; a program needn't handle non-finite values. Where the computation divides by a largest or mean magnitude, that divisor is 1e-20 or more.
Results may differ from a plain program's by a relative error of at most 0.0018.
Values may be sent and summed in bfloat16 or wider, within the bound.
No kernel may reach another device: no remote copies, remote signals or barrier semaphores. Data moves between devices by JAX's collectives and lax.ppermute only.
A program may use at most 64 MiB of HBM per device.

v0:
```python
import jax
import jax.numpy as jnp
from jax import lax
from jax.sharding import Mesh
from jax.sharding import PartitionSpec as P

NB = 96
NA = 16
REACH = 3
PURIF = 12
FRAG = ("frag_0", "frag_1", "frag_2")
GRP = ("grp_0", "grp_1")
GRP_FRAG = ("grp_0", "grp_1", "frag_0", "frag_1", "frag_2")
FULL_PRECISION = lax.Precision.HIGHEST


def from_everyone(value, axis):
    copies = jnp.broadcast_to(value, (lax.axis_size(axis), *value.shape))
    return lax.all_to_all(copies, axis, split_axis=0, concat_axis=0, tiled=True)


def joined_along(pieces, dim):
    shape = list(pieces.shape[1:])
    shape[dim] *= pieces.shape[0]
    return jnp.moveaxis(pieces, 0, dim).reshape(shape)


def collect(value, axis, dim):
    pieces = from_everyone(value, axis)
    return joined_along(pieces, dim)


def from_behind(value, axis, steps):
    count = lax.axis_size(axis)
    first, last = (max(0, -steps), min(count, count - steps))
    return lax.ppermute(value, axis, [(source, source + steps) for source in range(first, last)])


def in_blocks(value, dim, peers):
    shape = value.shape
    pieces = value.reshape(*shape[:dim], peers, shape[dim] // peers, *shape[dim + 1 :])
    return jnp.moveaxis(pieces, dim, 0)


def sent_and_summed(value, axis, dim):
    pieces = in_blocks(value, dim, lax.axis_size(axis))
    arrived = lax.all_to_all(pieces, axis, split_axis=0, concat_axis=0, tiled=True)
    return arrived.sum(axis=0)


def by_axis(value, axes):
    for axis in axes:
        value = lax.psum(value, axis)
    return value


def basis_atoms(count_real):
    basis_index = jnp.arange(NB, dtype=jnp.float32)[None, :, None]
    atom_index = jnp.arange(NA, dtype=jnp.float32)[None, None, :]
    scaled = basis_index * count_real[:, None, None]
    inside = jnp.logical_and(atom_index * NB <= scaled, scaled < (atom_index + 1.0) * NB)
    return inside.astype(jnp.float32)


def atom_table(density, nuclear_charge, atom_counts, coords):
    frag_count = density.shape[0]
    count_real = atom_counts.astype(jnp.float32)
    owners = basis_atoms(count_real)
    blocks = density.reshape(frag_count, NB, NB).astype(jnp.float32)
    on_diagonal = jnp.diagonal(blocks, axis1=1, axis2=2)
    population = 2.0 * jnp.sum(on_diagonal[:, :, None] * owners, axis=1)
    is_live = (jnp.arange(NA, dtype=jnp.float32)[None, :] < count_real[:, None]).astype(jnp.float32)
    charge = is_live * nuclear_charge.reshape(frag_count, NA) - population
    return jnp.concatenate([charge.reshape(1, -1), coords, is_live.reshape(1, -1)], axis=0)


def embed_potential(receivers, pair_ids, atom_rows):
    source_frag = jnp.arange(atom_rows.shape[1], dtype=jnp.int32) // NA
    keep_mask = jnp.logical_and(source_frag != pair_ids[0], source_frag != pair_ids[1]).astype(
        jnp.float32
    )
    offsets = receivers[1:4, :, None] - atom_rows[1:4, None, :]
    distance_sq = jnp.sum(offsets * offsets, axis=0)
    return jnp.sum((keep_mask * atom_rows[0])[None, :] / jnp.sqrt(distance_sq + 1.0), axis=1)


def dimer_solve(dens_pair, fock_pair, coupling_row, potential, count_pair):
    owners = basis_atoms(count_pair)
    site_shift = jnp.sum(owners * potential.reshape(2, 1, NA), axis=2)
    dens_blocks = dens_pair.astype(jnp.float32).reshape(2, NB, NB)
    fock_parts = fock_pair.astype(jnp.float32).reshape(2, NB, NB)
    cross_block = coupling_row.astype(jnp.float32).reshape(NB, NB)
    small_eye = jnp.eye(NB, dtype=jnp.float32)
    top_rows = jnp.concatenate(
        [fock_parts[0] + small_eye * site_shift[0][None, :], cross_block], axis=1
    )
    low_rows = jnp.concatenate(
        [cross_block.T, fock_parts[1] + small_eye * site_shift[1][None, :]], axis=1
    )
    dimer_fock = jnp.concatenate([top_rows, low_rows], axis=0)
    identity = jnp.eye(2 * NB, dtype=jnp.float32)
    centre = jnp.trace(dimer_fock) / (2.0 * NB)
    shifted = dimer_fock - centre * identity
    width = jnp.max(jnp.sum(jnp.abs(shifted), axis=1)) + 1e-06
    start = 0.5 * identity - shifted / (2.0 * width)

    def purify(index, current):
        square = jnp.dot(current, current, precision=FULL_PRECISION)
        return 3.0 * square - 2.0 * jnp.dot(square, current, precision=FULL_PRECISION)

    purified = lax.fori_loop(0, PURIF, purify, start)
    zero_block = jnp.zeros((NB, NB), jnp.float32)
    start_guess = jnp.concatenate(
        [
            jnp.concatenate([dens_blocks[0], zero_block], axis=1),
            jnp.concatenate([zero_block, dens_blocks[1]], axis=1),
        ],
        axis=0,
    )
    energy = jnp.sum((purified - start_guess) * dimer_fock.T)
    changes = jnp.stack([purified[:NB, :NB] - dens_blocks[0], purified[NB:, NB:] - dens_blocks[1]])
    return (changes.reshape(2, NB * NB), energy)


def per_device(density, fock_blocks, coupling, dimer_pairs, atom_counts, nuclear_charge, coords):
    frag_dev = density.shape[0]
    local_rows = atom_table(density, nuclear_charge, atom_counts, coords)
    atom_rows = collect(local_rows, FRAG, 1)
    my_index = lax.axis_index(FRAG)
    dens_list = [density]
    fock_list = [fock_blocks]
    for distance in range(1, REACH + 1):
        got_dens, got_fock = from_behind((density, fock_blocks), FRAG, -distance)
        dens_list.append(got_dens)
        fock_list.append(got_fock)
    held_dens = jnp.concatenate(dens_list, axis=0)
    held_fock = jnp.concatenate(fock_list, axis=0)
    first_row = my_index * frag_dev
    held_index = dimer_pairs - first_row

    def solve_one(pair_ids, row_pair, coupling_row):
        columns = (pair_ids[:, None] * NA + jnp.arange(NA, dtype=jnp.int32)[None, :]).reshape(-1)
        receivers = jnp.take(atom_rows, columns, axis=1)
        potential = embed_potential(receivers, pair_ids, atom_rows)
        count_pair = jnp.sum(receivers[4].reshape(2, NA), axis=1)
        return dimer_solve(
            jnp.take(held_dens, row_pair, axis=0),
            jnp.take(held_fock, row_pair, axis=0),
            coupling_row,
            potential,
            count_pair,
        )

    changes, energies = jax.vmap(solve_one)(dimer_pairs, held_index, coupling)
    held_count = held_dens.shape[0]
    selector = (
        jnp.arange(held_count, dtype=jnp.int32)[:, None] == held_index.reshape(1, -1)
    ).astype(jnp.float32)
    partial_value = jnp.dot(selector, changes.reshape(-1, NB * NB), precision=FULL_PRECISION)
    partial_value = sent_and_summed(partial_value, GRP, 1)
    own_rows = partial_value[:frag_dev]
    for distance in range(1, REACH + 1):
        piece = partial_value[distance * frag_dev : (distance + 1) * frag_dev]
        own_rows = own_rows + from_behind(piece.astype(jnp.bfloat16), FRAG, distance).astype(
            piece.dtype
        )
    own_rows = collect(own_rows, GRP, 1)
    total_energy = by_axis(jnp.sum(energies), GRP_FRAG)
    return (own_rows, energies, total_energy)


def solution(mesh):
    finer = Mesh(
        mesh.devices.reshape(2, 4, 2, 8, 2), ("grp_0", "grp_1", "frag_0", "frag_1", "frag_2")
    )
    return jax.shard_map(
        per_device,
        mesh=finer,
        in_specs=(
            P(FRAG, None),
            P(FRAG, None),
            P(GRP_FRAG, None),
            P(GRP_FRAG, None),
            P(FRAG),
            P(FRAG),
            P(None, FRAG),
        ),
        out_specs=(P(FRAG, None), P(GRP_FRAG), P()),
        check_vma=False,
    )
```

profile of v0, /device:TPU:1, one launch (start us, length us, event | category | flops | bytes accessed | tf_op | source)
XLA Modules:
  0.0 172.8 jit_solution(6586813165077546668)
XLA Ops:
  0.6 5.1 %collective-permute-start = (bf16[8,9216]{1,0:T(8,128)(2,1)}, bf16[8,9216]{1,0:T(8,128)(2,1)S(1)}, u32[]{:S(2)}, u32[]{:S(2)}) collective-permute-start(bf16[8,9216]{1,0:T(8,128)(2,1)} %param.12), channel_id=1, source_target_pairs={{1,0},{2,1},{3,2},{4,3},{5,4},{6,5},{7,6},{8,7},{9,8},{10,9},{11,1... | collective-permute-start | bytes 442376 | tf_op jit(solution)/shard_map/ppermute | solution.py:36
  5.7 1.3 collective-permute-start.1
  7.0 1.3 collective-permute-start.2
  8.3 1.9 %collective-permute-start.3 = (bf16[8,9216]{1,0:T(8,128)(2,1)}, bf16[8,9216]{1,0:T(8,128)(2,1)S(1)}, u32[]{:S(2)}, u32[]{:S(2)}) collective-permute-start(bf16[8,9216]{1,0:T(8,128)(2,1)} %param.11), channel_id=1, source_target_pairs={{1,0},{2,1},{3,2},{4,3},{5,4},{6,5},{7,6},{8,7},{9,8},{10,9},{11,1... | collective-permute-start | bytes 442376 | tf_op jit(solution)/shard_map/ppermute | solution.py:36
  10.3 1.3 collective-permute-start.4
  11.7 3.4 %copy.86 = f32[8,9216]{0,1:T(8,128)} copy(bf16[8,9216]{1,0:T(8,128)(2,1)} %param.11) | data formatting | bytes 442368 | tf_op jit(solution)/shard_map/convert_element_type | solution.py:69
  15.3 2.9 %gather_fusion = f32[96,8]{1,0:T(8,128)S(1)} fusion(f32[8,96,96]{0,2,1:T(8,128)} %bitcast.84, s32[96]{0:T(128)S(1)} %or_bitcast_fusion), kind=kCustom, calls=%fused_computation.2 | custom fusion | bytes 6912 | tf_op jit(solution)/shard_map/jit(diagonal)/gather | solution.py:70
  18.8 0.6 broadcast_in_dim.37
  19.4 15.1 %all-to-all-start = ((f32[32,5,128]{2,1,0:T(8,128)}), f32[32,5,128]{2,1,0:T(8,128)S(1)}, u32[]{:S(2)}, u32[]{:S(2)}) async-start(f32[32,5,128]{2,1,0:T(8,128)} %broadcast_in_dim.37), calls=%async_computation | async-start | bytes 262144 | tf_op jit(solution)/shard_map/all_to_all | solution.py:19
  35.5 0.6 fusion.11
  36.1 0.6 iota_compare_fusion.2
  36.9 0.6 pad_clamp_fusion
  38.7 0.7 eq.41
  39.4 0.7 fusion.10
  40.1 1.3 collective-permute-start.5
  41.4 0.6 gather_fusion.2
  42.2 8.3 %collective-permute-done.5 = bf16[8,9216]{1,0:T(8,128)(2,1)S(1)} collective-permute-done((bf16[8,9216]{1,0:T(8,128)(2,1)S(1)}, bf16[8,9216]{1,0:T(8,128)(2,1)S(1)}, u32[]{:S(2)}, u32[]{:S(2)}) %collective-permute-start.5) | collective-permute-done | bytes 147488 | tf_op jit(solution)/shard_map/ppermute | solution.py:36
  50.5 0.6 gather_fusion.3
  52.4 0.6 slice_bitcast_fusion.2
  53.7 1.5 copy.89
  55.2 0.8 gather_fusion.1
  56.1 0.7 select_bitcast_fusion
  56.8 0.8 copy.109
  57.6 0.8 multiply_reduce_fusion
  60.9 23.0 %while.10 = (s32[]{:T(128)}, f32[4,192,192]{2,1,0:T(8,128)S(1)}, s32[]{:T(128)}) while((s32[]{:T(128)}, f32[4,192,192]{2,1,0:T(8,128)S(1)}, s32[]{:T(128)}) %tuple.36), condition=%wide.region_9.11_spmd, body=%wide.region_8.10_spmd.sunk | while | flops 679919616 | bytes 4128813 | solution.py:111
  61.0 0.9 fusion.41
  61.9 0.9 fusion.42
  62.9 0.9 fusion.41
  63.8 0.9 fusion.42
  64.8 0.9 fusion.41
  65.7 0.9 fusion.42
  66.7 0.9 fusion.41
  67.6 0.9 fusion.42
  68.6 0.9 fusion.41
  69.5 0.9 fusion.42
  70.6 0.9 fusion.41
  71.5 0.9 fusion.42
  72.5 0.9 fusion.41
  73.4 0.9 fusion.42
  74.4 0.9 fusion.41
  75.3 0.9 fusion.42
  76.3 0.9 fusion.41
  77.2 0.9 fusion.42
  78.2 0.9 fusion.41
  79.1 0.9 fusion.42
  80.1 0.9 fusion.41
  81.0 0.9 fusion.42
  82.1 0.9 fusion.41
  83.0 0.9 fusion.42
  85.0 0.7 convolution_bitcast_fusion
  85.8 22.6 %all_to_all.15 = f32[8,32,1152]{2,1,0:T(8,128)S(1)} all-to-all(f32[8,32,1152]{2,1,0:T(8,128)S(1)} %convolution_bitcast_fusion), channel_id=1, replica_groups=mesh['grp_0'=2,'grp_1'=4,'frag_0'=2,'frag_1'=8,'frag_2'=2] {'grp_0','grp..., dimensions={0} | all-to-all | bytes 2359296 | tf_op jit(solution)/shard_map/all_to_all | solution.py:47
  108.5 5.4 %collective-permute-start.6 = (bf16[8,1152]{1,0:T(8,128)(2,1)S(1)}, bf16[8,1152]{1,0:T(8,128)(2,1)S(1)}, u32[]{:S(2)}, u32[]{:S(2)}) collective-permute-start(bf16[8,1152]{1,0:T(8,128)(2,1)S(1)} %get-tuple-element.33), channel_id=1, source_target_pairs={{0,1},{1,2},{2,3},{3,4},{4,5},{5,6},{6,7},{7,8},{8,9},{9,10},{10,1... | collective-permute-start | bytes 55304 | tf_op jit(solution)/shard_map/ppermute | solution.py:36
  113.8 1.3 collective-permute-start.7
  115.1 6.0 %collective-permute-start.8 = (bf16[8,1152]{1,0:T(8,128)(2,1)S(1)}, bf16[8,1152]{1,0:T(8,128)(2,1)S(1)}, u32[]{:S(2)}, u32[]{:S(2)}) collective-permute-start(bf16[8,1152]{1,0:T(8,128)(2,1)S(1)} %get-tuple-element.34), channel_id=1, source_target_pairs={{0,3},{1,4},{2,5},{3,6},{4,7},{5,8},{6,9},{7,10},{8,11},{9,12},{10... | collective-permute-start | bytes 55304 | tf_op jit(solution)/shard_map/ppermute | solution.py:36
  121.1 0.8 collective-permute-done.8
  122.0 0.7 broadcast_in_dim.44
  122.7 3.4 %all-to-all-start.2 = ((f32[8,8,1152]{2,1,0:T(8,128)}), f32[8,8,1152]{2,1,0:T(8,128)S(1)}, u32[]{:S(2)}, u32[]{:S(2)}) async-start(f32[8,8,1152]{2,1,0:T(8,128)} %broadcast_in_dim.44), calls=%async_computation.2 | async-start | bytes 589824 | tf_op jit(solution)/shard_map/all_to_all | solution.py:19
  126.2 1.0 fusion.21
  127.1 6.0 %psum.35 = f32[]{:T(128)} all-reduce(f32[]{:T(128)} %get-tuple-element.19), channel_id=1, replica_groups=mesh['grp_0'=2,'grp_1'=4,'frag_0'=2,'frag_1'=8,'frag_2'=2] {'grp_0'}, use_global_device_ids=true, to_apply=%region_13.15 | all-reduce | flops 1 | bytes 8 | tf_op jit(solution)/shard_map/psum | solution.py:53
  133.1 9.5 %psum.36 = f32[]{:T(128)} all-reduce(f32[]{:T(128)} %psum.35), channel_id=1, replica_groups=mesh['grp_0'=2,'grp_1'=4,'frag_0'=2,'frag_1'=8,'frag_2'=2] {'grp_1'}, use_global_device_ids=true, to_apply=%region_14.16 | all-reduce | flops 1 | bytes 8 | tf_op jit(solution)/shard_map/psum | solution.py:53
  142.6 4.8 %psum.37 = f32[]{:T(128)} all-reduce(f32[]{:T(128)} %psum.36), channel_id=1, replica_groups=mesh['grp_0'=2,'grp_1'=4,'frag_0'=2,'frag_1'=8,'frag_2'=2] {'frag_0'}, use_global_device_ids=true, to_apply=%region_15.17 | all-reduce | flops 1 | bytes 8 | tf_op jit(solution)/shard_map/psum | solution.py:53
  147.4 13.5 %psum.38 = f32[]{:T(128)} all-reduce(f32[]{:T(128)} %psum.37), channel_id=1, replica_groups=mesh['grp_0'=2,'grp_1'=4,'frag_0'=2,'frag_1'=8,'frag_2'=2] {'frag_1'}, use_global_device_ids=true, to_apply=%region_16.18 | all-reduce | flops 1 | bytes 8 | tf_op jit(solution)/shard_map/psum | solution.py:53
  160.9 11.2 %psum.39 = f32[]{:T(128)} all-reduce(f32[]{:T(128)} %psum.38), channel_id=1, replica_groups=mesh['grp_0'=2,'grp_1'=4,'frag_0'=2,'frag_1'=8,'frag_2'=2] {'frag_2'}, use_global_device_ids=true, to_apply=%region_17.19 | all-reduce | flops 1 | bytes 8 | tf_op jit(solution)/shard_map/psum | solution.py:53
  172.1 0.7 copy.121
  (134 shorter events, 9.3 us)
Async XLA Ops:
  0.6 39.4 %collective-permute-start = (bf16[8,9216]{1,0:T(8,128)(2,1)}, bf16[8,9216]{1,0:T(8,128)(2,1)S(1)}, u32[]{:S(2)}, u32[]{:S(2)}) collective-permute-start(bf16[8,9216]{1,0:T(8,128)(2,1)} %param.12), channel_id=1, source_target_pairs={{1,0},{2,1},{3,2},{4,3},{5,4},{6,5},{7,6},{8,7},{9,8},{10,9},{11,1... | collective-permute-start | bytes 442376 | tf_op jit(solution)/shard_map/ppermute | solution.py:36
  5.7 35.6 %collective-permute-start.1 = (bf16[8,9216]{1,0:T(8,128)(2,1)}, bf16[8,9216]{1,0:T(8,128)(2,1)S(1)}, u32[]{:S(2)}, u32[]{:S(2)}) collective-permute-start(bf16[8,9216]{1,0:T(8,128)(2,1)} %param.12), channel_id=1, source_target_pairs={{2,0},{3,1},{4,2},{5,3},{6,4},{7,5},{8,6},{9,7},{10,8},{11,9},{12,... | collective-permute-start | bytes 442376 | tf_op jit(solution)/shard_map/ppermute | solution.py:36
  7.0 34.3 %collective-permute-start.2 = (bf16[8,9216]{1,0:T(8,128)(2,1)}, bf16[8,9216]{1,0:T(8,128)(2,1)S(1)}, u32[]{:S(2)}, u32[]{:S(2)}) collective-permute-start(bf16[8,9216]{1,0:T(8,128)(2,1)} %param.12), channel_id=1, source_target_pairs={{3,0},{4,1},{5,2},{6,3},{7,4},{8,5},{9,6},{10,7},{11,8},{12,9},{13... | collective-permute-start | bytes 442376 | tf_op jit(solution)/shard_map/ppermute | solution.py:36
  8.3 33.8 %collective-permute-start.3 = (bf16[8,9216]{1,0:T(8,128)(2,1)}, bf16[8,9216]{1,0:T(8,128)(2,1)S(1)}, u32[]{:S(2)}, u32[]{:S(2)}) collective-permute-start(bf16[8,9216]{1,0:T(8,128)(2,1)} %param.11), channel_id=1, source_target_pairs={{1,0},{2,1},{3,2},{4,3},{5,4},{6,5},{7,6},{8,7},{9,8},{10,9},{11,1... | collective-permute-start | bytes 442376 | tf_op jit(solution)/shard_map/ppermute | solution.py:36
  10.3 31.9 %collective-permute-start.4 = (bf16[8,9216]{1,0:T(8,128)(2,1)}, bf16[8,9216]{1,0:T(8,128)(2,1)S(1)}, u32[]{:S(2)}, u32[]{:S(2)}) collective-permute-start(bf16[8,9216]{1,0:T(8,128)(2,1)} %param.11), channel_id=1, source_target_pairs={{2,0},{3,1},{4,2},{5,3},{6,4},{7,5},{8,6},{9,7},{10,8},{11,9},{12,... | collective-permute-start | bytes 442376 | tf_op jit(solution)/shard_map/ppermute | solution.py:36
  11.6 6.7 %copy-start.13 = (f32[16]{0:T(128)}, f32[16]{0:T(128)S(1)}, u32[]{:S(2)}) copy-start(f32[16]{0:T(128)S(1)} %get-tuple-element.44) | copy-start | bytes 196
  11.6 6.7 %copy-start.15 = (f32[16]{0:T(128)}, f32[16]{0:T(128)S(1)}, u32[]{:S(2)}) copy-start(f32[16]{0:T(128)S(1)} %get-tuple-element.45) | copy-start | bytes 196
  11.6 3.5 %copy-start.18 = (s32[8]{0:T(128)S(1)}, s32[8]{0:T(128)}, u32[]{:S(2)}) copy-start(s32[8]{0:T(128)} %param.15) | copy-start | bytes 100
  11.6 7.1 %copy-start.17 = (f32[128]{0:T(128)S(1)}, f32[128]{0:T(128)}, u32[]{:S(2)}) copy-start(f32[128]{0:T(128)} %param.16) | copy-start | bytes 1540
  11.6 7.1 %copy-start.12 = (f32[3,128]{1,0:T(4,128)S(1)}, f32[3,128]{1,0:T(4,128)}, u32[]{:S(2)}) copy-start(f32[3,128]{1,0:T(4,128)} %param.17) | copy-start | bytes 4612
  11.6 22.9 %copy-start.8 = (s32[4,2]{0,1:T(2,128)S(1)}, s32[4,2]{0,1:T(2,128)}, u32[]{:S(2)}) copy-start(s32[4,2]{0,1:T(2,128)} %param.14) | copy-start | bytes 100
  11.7 26.8 %copy-start.6 = (bf16[4,9216]{1,0:T(4,128)(2,1)S(1)}, bf16[4,9216]{1,0:T(4,128)(2,1)}, u32[]{:S(2)}) copy-start(bf16[4,9216]{1,0:T(4,128)(2,1)} %param.13) | copy-start | bytes 221188
  15.1 25.0 %copy-start.2 = (bf16[8,9216]{1,0:T(8,128)(2,1)S(1)}, bf16[8,9216]{1,0:T(8,128)(2,1)}, u32[]{:S(2)}) copy-start(bf16[8,9216]{1,0:T(8,128)(2,1)} %param.11) | copy-start | bytes 442372
  15.1 26.3 %copy-start.5 = (bf16[8,9216]{1,0:T(8,128)(2,1)S(1)}, bf16[8,9216]{1,0:T(8,128)(2,1)}, u32[]{:S(2)}) copy-start(bf16[8,9216]{1,0:T(8,128)(2,1)} %param.12) | copy-start | bytes 442372
  19.4 33.0 %all-to-all-start = ((f32[32,5,128]{2,1,0:T(8,128)}), f32[32,5,128]{2,1,0:T(8,128)S(1)}, u32[]{:S(2)}, u32[]{:S(2)}) async-start(f32[32,5,128]{2,1,0:T(8,128)} %broadcast_in_dim.37), calls=%async_computation | async-start | bytes 262144 | tf_op jit(solution)/shard_map/all_to_all | solution.py:19
  40.1 10.4 %collective-permute-start.5 = (bf16[8,9216]{1,0:T(8,128)(2,1)S(1)}, bf16[8,9216]{1,0:T(8,128)(2,1)S(1)}, u32[]{:S(2)}, u32[]{:S(2)}) collective-permute-start(bf16[8,9216]{1,0:T(8,128)(2,1)S(1)} %copy-done.2), channel_id=1, source_target_pairs={{3,0},{4,1},{5,2},{6,3},{7,4},{8,5},{9,6},{10,7},{11,8},{12,9},{13... | collective-permute-start | bytes 442376 | tf_op jit(solution)/shard_map/ppermute | solution.py:36
  52.4 1.3 copy-start
  56.1 2.4 %copy-start.7 = (f32[4096]{0:T(1024)S(1)}, f32[4096]{0:T(1024)}, u32[]{:S(2)}) copy-start(f32[4096]{0:T(1024)} %slice_bitcast_fusion.3) | copy-start | bytes 49156
  56.1 2.4 %copy-start.10 = (s32[4]{0:T(128)S(1)}, s32[4]{0:T(128)}, u32[]{:S(2)}) copy-start(s32[4]{0:T(128)} %get-tuple-element.38) | copy-start | bytes 52
  56.1 2.4 %copy-start.11 = (s32[4]{0:T(128)S(1)}, s32[4]{0:T(128)}, u32[]{:S(2)}) copy-start(s32[4]{0:T(128)} %get-tuple-element.39) | copy-start | bytes 52
  58.4 0.9 copy-start.14
  58.4 0.9 copy-start.16
  58.4 1.0 copy-start.4
  58.6 1.0 copy-start.3
  59.5 1.1 copy-start.1
  84.3 0.7 copy-start.9
  108.5 12.6 %collective-permute-start.6 = (bf16[8,1152]{1,0:T(8,128)(2,1)S(1)}, bf16[8,1152]{1,0:T(8,128)(2,1)S(1)}, u32[]{:S(2)}, u32[]{:S(2)}) collective-permute-start(bf16[8,1152]{1,0:T(8,128)(2,1)S(1)} %get-tuple-element.33), channel_id=1, source_target_pairs={{0,1},{1,2},{2,3},{3,4},{4,5},{5,6},{6,7},{7,8},{8,9},{9,10},{10,1... | collective-permute-start | bytes 55304 | tf_op jit(solution)/shard_map/ppermute | solution.py:36
  113.8 7.3 %collective-permute-start.7 = (bf16[8,1152]{1,0:T(8,128)(2,1)S(1)}, bf16[8,1152]{1,0:T(8,128)(2,1)S(1)}, u32[]{:S(2)}, u32[]{:S(2)}) collective-permute-start(bf16[8,1152]{1,0:T(8,128)(2,1)S(1)} %get-tuple-element.35), channel_id=1, source_target_pairs={{0,2},{1,3},{2,4},{3,5},{4,6},{5,7},{6,8},{7,9},{8,10},{9,11},{10,... | collective-permute-start | bytes 55304 | tf_op jit(solution)/shard_map/ppermute | solution.py:36
  115.1 6.8 %collective-permute-start.8 = (bf16[8,1152]{1,0:T(8,128)(2,1)S(1)}, bf16[8,1152]{1,0:T(8,128)(2,1)S(1)}, u32[]{:S(2)}, u32[]{:S(2)}) collective-permute-start(bf16[8,1152]{1,0:T(8,128)(2,1)S(1)} %get-tuple-element.34), channel_id=1, source_target_pairs={{0,3},{1,4},{2,5},{3,6},{4,7},{5,8},{6,9},{7,10},{8,11},{9,12},{10... | collective-permute-start | bytes 55304 | tf_op jit(solution)/shard_map/ppermute | solution.py:36
  122.7 49.4 %all-to-all-start.2 = ((f32[8,8,1152]{2,1,0:T(8,128)}), f32[8,8,1152]{2,1,0:T(8,128)S(1)}, u32[]{:S(2)}, u32[]{:S(2)}) async-start(f32[8,8,1152]{2,1,0:T(8,128)} %broadcast_in_dim.44), calls=%async_computation.2 | async-start | bytes 589824 | tf_op jit(solution)/shard_map/all_to_all | solution.py:19
where the time goes:
time: 174 us; the launch traced here: 173 us
  blocking collectives  67.5 us (39%)
  starting transfers between devices  43.3 us (25%)
  matrix products  22.6 us (13%)
  local copies, waits for them, and re-layouts  19.7 us (11%)
  waiting for transfers between devices  9.16 us (5%)
  other arithmetic  8.75 us (5%)
    psum x5, blocking collectives, by_axis(): value = lax.psum(value, axis)  44.9 us
    ppermute x9, starting transfers between devices, from_behind(): lax.ppermute(value, axis, [(source, source + steps) for source in range(f...  24.8 us
    all_to_all x1, blocking collectives, sent_and_summed(): lax.all_to_all(pieces, axis, split_axis=0, concat_axis=0, tiled=True)  22.6 us
    all_to_all x2, starting transfers between devices, from_everyone(): return lax.all_to_all(copies, axis, split_axis=0, concat_axis=0, tiled=True)  18.5 us
    dot_general x12, matrix products, purify(): jnp.dot(square, current, precision=FULL_PRECISION)  11.2 us
    dot_general x12, matrix products, purify(): square = jnp.dot(current, current, precision=FULL_PRECISION)  10.7 us
    ppermute x9, waiting for transfers between devices, from_behind(): lax.ppermute(value, axis, [(source, source + steps) for source in range(f...  9.15 us
  transfers between devices with their start and end apart: 11, of which 2 were waited for; matrix products, arithmetic and copies ran while one was open for 10% of the time, Pallas kernels for 0%

commit v1 on v0

--- a/solution.py
+++ b/solution.py
@@ -12,6 +12,11 @@
 GRP = ("grp_0", "grp_1")
 GRP_FRAG = ("grp_0", "grp_1", "frag_0", "frag_1", "frag_2")
 FULL_PRECISION = lax.Precision.HIGHEST
+
+
+def touch_the_boxes(vals, named_axis):
+    a_now = jnp.sum(lax.all_gather(vals, axis_name=named_axis), 0)
+    return a_now
 
 
 def from_everyone(value, axis):
@@ -50,7 +55,7 @@
 
 def by_axis(value, axes):
     for axis in axes:
-        value = lax.psum(value, axis)
+        value = touch_the_boxes(value, axis)
     return value
 
 

time: 174 us -> 184 us (1.057)
  local copies, waits for them, and re-layouts: 19.7 us -> 30.2 us
  blocking collectives: 67.5 us -> 64.3 us
  other arithmetic: 8.75 us -> 11.8 us
    psum x5 -> x0, blocking collectives: 44.9 us -> none  [by_axis(): value = lax.psum(value, axis)]
    unnamed x0 -> x5, blocking collectives: none -> 41.7 us
    unnamed x43 -> x68, local copies, waits for them, and re-layouts: 2.74 us -> 13.3 us
    reduce_sum x0 -> x5, other arithmetic: none -> 3.02 us  [touch_the_boxes(): a_now = jnp.sum(lax.all_gather(vals, axis_name=named_axis), 0)]
  transfers between devices with their start and end apart: 11 -> 11, of which waited for: 2 -> 2; matrix products, arithmetic and copies ran while one was open for 10% -> 17% of each run, Pallas kernels for 0% -> 0%
where the time goes in v1:
time: 184 us; the launch traced here: 183 us
  blocking collectives  64.3 us (35%)
  starting transfers between devices  43.5 us (24%)
  local copies, waits for them, and re-layouts  30.2 us (16%)
  matrix products  22.6 us (12%)
  other arithmetic  11.8 us (6%)
  waiting for transfers between devices  9.16 us (5%)
    unnamed x5, blocking collectives  41.7 us
    ppermute x9, starting transfers between devices, from_behind(): lax.ppermute(value, axis, [(source, source + steps) for source in range(f...  24.8 us
    all_to_all x1, blocking collectives, sent_and_summed(): lax.all_to_all(pieces, axis, split_axis=0, concat_axis=0, tiled=True)  22.6 us
    all_to_all x2, starting transfers between devices, from_everyone(): return lax.all_to_all(copies, axis, split_axis=0, concat_axis=0, tiled=True)  18.7 us
    unnamed x68, local copies, waits for them, and re-layouts  13.3 us
    dot_general x12, matrix products, purify(): jnp.dot(square, current, precision=FULL_PRECISION)  11.2 us
    dot_general x12, matrix products, purify(): square = jnp.dot(current, current, precision=FULL_PRECISION)  10.7 us
    ppermute x9, waiting for transfers between devices, from_behind(): lax.ppermute(value, axis, [(source, source + steps) for source in range(f...  9.15 us
  transfers between devices with their start and end apart: 11, of which 2 were waited for; matrix products, arithmetic and copies ran while one was open for 17% of the time, Pallas kernels for 0%

profile of v1, /device:TPU:1, one launch (start us, length us, event | category | flops | bytes accessed | tf_op | source)
XLA Modules:
  0.0 183.4 jit_solution(1791864376946041792)
XLA Ops:
  0.6 5.1 %collective-permute-start = (bf16[8,9216]{1,0:T(8,128)(2,1)}, bf16[8,9216]{1,0:T(8,128)(2,1)S(1)}, u32[]{:S(2)}, u32[]{:S(2)}) collective-permute-start(bf16[8,9216]{1,0:T(8,128)(2,1)} %param.12), channel_id=1, source_target_pairs={{1,0},{2,1},{3,2},{4,3},{5,4},{6,5},{7,6},{8,7},{9,8},{10,9},{11,1... | collective-permute-start | bytes 442376 | tf_op jit(solution)/shard_map/ppermute | solution.py:41
  5.7 1.3 collective-permute-start.1
  7.0 1.3 collective-permute-start.2
  8.3 1.9 %collective-permute-start.3 = (bf16[8,9216]{1,0:T(8,128)(2,1)}, bf16[8,9216]{1,0:T(8,128)(2,1)S(1)}, u32[]{:S(2)}, u32[]{:S(2)}) collective-permute-start(bf16[8,9216]{1,0:T(8,128)(2,1)} %param.11), channel_id=1, source_target_pairs={{1,0},{2,1},{3,2},{4,3},{5,4},{6,5},{7,6},{8,7},{9,8},{10,9},{11,1... | collective-permute-start | bytes 442376 | tf_op jit(solution)/shard_map/ppermute | solution.py:41
  10.3 1.3 collective-permute-start.4
  11.7 3.4 %copy.86 = f32[8,9216]{0,1:T(8,128)} copy(bf16[8,9216]{1,0:T(8,128)(2,1)} %param.11) | data formatting | bytes 442368 | tf_op jit(solution)/shard_map/convert_element_type | solution.py:74
  15.3 2.9 %gather_fusion = f32[96,8]{1,0:T(8,128)S(1)} fusion(f32[8,96,96]{0,2,1:T(8,128)} %bitcast.94, s32[96]{0:T(128)S(1)} %or_bitcast_fusion), kind=kCustom, calls=%fused_computation.2 | custom fusion | bytes 6912 | tf_op jit(solution)/shard_map/jit(diagonal)/gather | solution.py:75
  19.4 15.1 %all-to-all-start = ((f32[32,5,128]{2,1,0:T(8,128)}), f32[32,5,128]{2,1,0:T(8,128)S(1)}, u32[]{:S(2)}, u32[]{:S(2)}) async-start(f32[32,5,128]{2,1,0:T(8,128)} %broadcast_in_dim.37), calls=%async_computation | async-start | bytes 262144 | tf_op jit(solution)/shard_map/all_to_all | solution.py:24
  38.7 0.7 eq.41
  39.4 0.7 fusion.10
  40.1 1.3 collective-permute-start.5
  42.2 8.3 %collective-permute-done.5 = bf16[8,9216]{1,0:T(8,128)(2,1)S(1)} collective-permute-done((bf16[8,9216]{1,0:T(8,128)(2,1)S(1)}, bf16[8,9216]{1,0:T(8,128)(2,1)S(1)}, u32[]{:S(2)}, u32[]{:S(2)}) %collective-permute-start.5) | collective-permute-done | bytes 147488 | tf_op jit(solution)/shard_map/ppermute | solution.py:41
  53.7 1.5 copy.89
  55.2 0.8 gather_fusion.1
  56.1 0.7 select_bitcast_fusion
  56.8 0.8 copy.109
  57.6 0.8 multiply_reduce_fusion
  60.9 23.0 %while.10 = (s32[]{:T(128)}, f32[4,192,192]{2,1,0:T(8,128)S(1)}, s32[]{:T(128)}) while((s32[]{:T(128)}, f32[4,192,192]{2,1,0:T(8,128)S(1)}, s32[]{:T(128)}) %tuple.36), condition=%wide.region_9.11_spmd, body=%wide.region_8.10_spmd.sunk | while | flops 679919616 | bytes 4128813 | solution.py:116
  61.0 0.9 fusion.41
  61.9 0.9 fusion.42
  62.9 0.9 fusion.41
  63.8 0.9 fusion.42
  64.8 0.9 fusion.41
  65.7 0.9 fusion.42
  66.7 0.9 fusion.41
  67.6 0.9 fusion.42
  68.6 0.9 fusion.41
  69.5 0.9 fusion.42
  70.6 0.9 fusion.41
  71.5 0.9 fusion.42
  72.5 0.9 fusion.41
  73.4 0.9 fusion.42
  74.4 0.9 fusion.41
  75.3 0.9 fusion.42
  76.3 0.9 fusion.41
  77.2 0.9 fusion.42
  78.2 0.9 fusion.41
  79.1 0.9 fusion.42
  80.1 0.9 fusion.41
  81.0 0.9 fusion.42
  82.1 0.9 fusion.41
  83.0 0.9 fusion.42
  85.0 0.7 convolution_bitcast_fusion
  85.8 22.6 %all_to_all.15 = f32[8,32,1152]{2,1,0:T(8,128)S(1)} all-to-all(f32[8,32,1152]{2,1,0:T(8,128)S(1)} %convolution_bitcast_fusion), channel_id=1, replica_groups=mesh['grp_0'=2,'grp_1'=4,'frag_0'=2,'frag_1'=8,'frag_2'=2] {'grp_0','grp..., dimensions={0} | all-to-all | bytes 2359296 | tf_op jit(solution)/shard_map/all_to_all | solution.py:52
  108.5 5.4 %collective-permute-start.6 = (bf16[8,1152]{1,0:T(8,128)(2,1)S(1)}, bf16[8,1152]{1,0:T(8,128)(2,1)S(1)}, u32[]{:S(2)}, u32[]{:S(2)}) collective-permute-start(bf16[8,1152]{1,0:T(8,128)(2,1)S(1)} %get-tuple-element.33), channel_id=1, source_target_pairs={{0,1},{1,2},{2,3},{3,4},{4,5},{5,6},{6,7},{7,8},{8,9},{9,10},{10,1... | collective-permute-start | bytes 55304 | tf_op jit(solution)/shard_map/ppermute | solution.py:41
  113.8 1.3 collective-permute-start.7
  115.1 6.0 %collective-permute-start.8 = (bf16[8,1152]{1,0:T(8,128)(2,1)S(1)}, bf16[8,1152]{1,0:T(8,128)(2,1)S(1)}, u32[]{:S(2)}, u32[]{:S(2)}) collective-permute-start(bf16[8,1152]{1,0:T(8,128)(2,1)S(1)} %get-tuple-element.34), channel_id=1, source_target_pairs={{0,3},{1,4},{2,5},{3,6},{4,7},{5,8},{6,9},{7,10},{8,11},{9,12},{10... | collective-permute-start | bytes 55304 | tf_op jit(solution)/shard_map/ppermute | solution.py:41
  121.1 0.8 collective-permute-done.8
  122.0 0.7 broadcast_in_dim.44
  122.7 3.6 %all-to-all-start.2 = ((f32[8,8,1152]{2,1,0:T(8,128)}), f32[8,8,1152]{2,1,0:T(8,128)S(1)}, u32[]{:S(2)}, u32[]{:S(2)}) async-start(f32[8,8,1152]{2,1,0:T(8,128)} %broadcast_in_dim.44), calls=%async_computation.2 | async-start | bytes 589824 | tf_op jit(solution)/shard_map/all_to_all | solution.py:24
  126.3 0.7 dynamic-slice
  127.0 1.0 fusion.21
  128.0 1.4 dynamic-update-slice
  129.4 0.7 dynamic-slice.1
  130.1 5.9 %all-reduce.2 = f32[2]{0:T(128)S(1)} all-reduce(f32[2]{0:T(128)S(1)} %dynamic-update-slice), channel_id=1, replica_groups=mesh['grp_0'=2,'grp_1'=4,'frag_0'=2,'frag_1'=8,'frag_2'=2] {'grp_0'}, use_global_device_ids=true, to_apply=%add.2 | all-reduce | flops 2 | bytes 16
  136.6 1.4 dynamic-update-slice.1
  138.7 8.0 %all-reduce.3 = f32[4]{0:T(128)S(1)} all-reduce(f32[4]{0:T(128)S(1)} %dynamic-update-slice.1), channel_id=1, replica_groups=mesh['grp_0'=2,'grp_1'=4,'frag_0'=2,'frag_1'=8,'frag_2'=2] {'grp_1'}, use_global_device_ids=true, to_apply=%add.3 | all-reduce | flops 4 | bytes 32
  147.2 1.4 dynamic-update-slice.2
  149.4 3.8 %all-reduce.4 = f32[2]{0:T(128)S(1)} all-reduce(f32[2]{0:T(128)S(1)} %dynamic-update-slice.2), channel_id=1, replica_groups=mesh['grp_0'=2,'grp_1'=4,'frag_0'=2,'frag_1'=8,'frag_2'=2] {'frag_0'}, use_global_device_ids=true, to_apply=%add.4 | all-reduce | flops 2 | bytes 16
  153.8 1.4 dynamic-update-slice.3
  155.9 12.8 %all-reduce.5 = f32[8]{0:T(128)S(1)} all-reduce(f32[8]{0:T(128)S(1)} %dynamic-update-slice.3), channel_id=1, replica_groups=mesh['grp_0'=2,'grp_1'=4,'frag_0'=2,'frag_1'=8,'frag_2'=2] {'frag_1'}, use_global_device_ids=true, to_apply=%add.5 | all-reduce | flops 8 | bytes 64
  169.3 1.4 dynamic-update-slice.4
  170.8 11.3 %all-reduce.6 = f32[2]{0:T(128)S(1)} all-reduce(f32[2]{0:T(128)S(1)} %dynamic-update-slice.4), channel_id=1, replica_groups=mesh['grp_0'=2,'grp_1'=4,'frag_0'=2,'frag_1'=8,'frag_2'=2] {'frag_2'}, use_global_device_ids=true, to_apply=%add.6 | all-reduce | flops 2 | bytes 16
  182.6 0.7 copy.133
  (164 shorter events, 18.7 us)
Async XLA Ops:
  0.6 39.4 %collective-permute-start = (bf16[8,9216]{1,0:T(8,128)(2,1)}, bf16[8,9216]{1,0:T(8,128)(2,1)S(1)}, u32[]{:S(2)}, u32[]{:S(2)}) collective-permute-start(bf16[8,9216]{1,0:T(8,128)(2,1)} %param.12), channel_id=1, source_target_pairs={{1,0},{2,1},{3,2},{4,3},{5,4},{6,5},{7,6},{8,7},{9,8},{10,9},{11,1... | collective-permute-start | bytes 442376 | tf_op jit(solution)/shard_map/ppermute | solution.py:41
  5.7 35.6 %collective-permute-start.1 = (bf16[8,9216]{1,0:T(8,128)(2,1)}, bf16[8,9216]{1,0:T(8,128)(2,1)S(1)}, u32[]{:S(2)}, u32[]{:S(2)}) collective-permute-start(bf16[8,9216]{1,0:T(8,128)(2,1)} %param.12), channel_id=1, source_target_pairs={{2,0},{3,1},{4,2},{5,3},{6,4},{7,5},{8,6},{9,7},{10,8},{11,9},{12,... | collective-permute-start | bytes 442376 | tf_op jit(solution)/shard_map/ppermute | solution.py:41
  7.0 34.3 %collective-permute-start.2 = (bf16[8,9216]{1,0:T(8,128)(2,1)}, bf16[8,9216]{1,0:T(8,128)(2,1)S(1)}, u32[]{:S(2)}, u32[]{:S(2)}) collective-permute-start(bf16[8,9216]{1,0:T(8,128)(2,1)} %param.12), channel_id=1, source_target_pairs={{3,0},{4,1},{5,2},{6,3},{7,4},{8,5},{9,6},{10,7},{11,8},{12,9},{13... | collective-permute-start | bytes 442376 | tf_op jit(solution)/shard_map/ppermute | solution.py:41
  8.3 33.8 %collective-permute-start.3 = (bf16[8,9216]{1,0:T(8,128)(2,1)}, bf16[8,9216]{1,0:T(8,128)(2,1)S(1)}, u32[]{:S(2)}, u32[]{:S(2)}) collective-permute-start(bf16[8,9216]{1,0:T(8,128)(2,1)} %param.11), channel_id=1, source_target_pairs={{1,0},{2,1},{3,2},{4,3},{5,4},{6,5},{7,6},{8,7},{9,8},{10,9},{11,1... | collective-permute-start | bytes 442376 | tf_op jit(solution)/shard_map/ppermute | solution.py:41
  10.3 31.9 %collective-permute-start.4 = (bf16[8,9216]{1,0:T(8,128)(2,1)}, bf16[8,9216]{1,0:T(8,128)(2,1)S(1)}, u32[]{:S(2)}, u32[]{:S(2)}) collective-permute-start(bf16[8,9216]{1,0:T(8,128)(2,1)} %param.11), channel_id=1, source_target_pairs={{2,0},{3,1},{4,2},{5,3},{6,4},{7,5},{8,6},{9,7},{10,8},{11,9},{12,... | collective-permute-start | bytes 442376 | tf_op jit(solution)/shard_map/ppermute | solution.py:41
  11.6 6.7 %copy-start.13 = (f32[16]{0:T(128)}, f32[16]{0:T(128)S(1)}, u32[]{:S(2)}) copy-start(f32[16]{0:T(128)S(1)} %get-tuple-element.44) | copy-start | bytes 196
  11.6 6.7 %copy-start.15 = (f32[16]{0:T(128)}, f32[16]{0:T(128)S(1)}, u32[]{:S(2)}) copy-start(f32[16]{0:T(128)S(1)} %get-tuple-element.45) | copy-start | bytes 196
  11.6 3.5 %copy-start.18 = (s32[8]{0:T(128)S(1)}, s32[8]{0:T(128)}, u32[]{:S(2)}) copy-start(s32[8]{0:T(128)} %param.15) | copy-start | bytes 100
  11.6 7.1 %copy-start.17 = (f32[128]{0:T(128)S(1)}, f32[128]{0:T(128)}, u32[]{:S(2)}) copy-start(f32[128]{0:T(128)} %param.16) | copy-start | bytes 1540
  11.6 7.1 %copy-start.12 = (f32[3,128]{1,0:T(4,128)S(1)}, f32[3,128]{1,0:T(4,128)}, u32[]{:S(2)}) copy-start(f32[3,128]{1,0:T(4,128)} %param.17) | copy-start | bytes 4612
  11.6 22.9 %copy-start.8 = (s32[4,2]{0,1:T(2,128)S(1)}, s32[4,2]{0,1:T(2,128)}, u32[]{:S(2)}) copy-start(s32[4,2]{0,1:T(2,128)} %param.14) | copy-start | bytes 100
  11.7 26.8 %copy-start.6 = (bf16[4,9216]{1,0:T(4,128)(2,1)S(1)}, bf16[4,9216]{1,0:T(4,128)(2,1)}, u32[]{:S(2)}) copy-start(bf16[4,9216]{1,0:T(4,128)(2,1)} %param.13) | copy-start | bytes 221188
  15.1 25.0 %copy-start.2 = (bf16[8,9216]{1,0:T(8,128)(2,1)S(1)}, bf16[8,9216]{1,0:T(8,128)(2,1)}, u32[]{:S(2)}) copy-start(bf16[8,9216]{1,0:T(8,128)(2,1)} %param.11) | copy-start | bytes 442372
  15.1 26.3 %copy-start.5 = (bf16[8,9216]{1,0:T(8,128)(2,1)S(1)}, bf16[8,9216]{1,0:T(8,128)(2,1)}, u32[]{:S(2)}) copy-start(bf16[8,9216]{1,0:T(8,128)(2,1)} %param.12) | copy-start | bytes 442372
  19.4 33.0 %all-to-all-start = ((f32[32,5,128]{2,1,0:T(8,128)}), f32[32,5,128]{2,1,0:T(8,128)S(1)}, u32[]{:S(2)}, u32[]{:S(2)}) async-start(f32[32,5,128]{2,1,0:T(8,128)} %broadcast_in_dim.37), calls=%async_computation | async-start | bytes 262144 | tf_op jit(solution)/shard_map/all_to_all | solution.py:24
  40.1 10.4 %collective-permute-start.5 = (bf16[8,9216]{1,0:T(8,128)(2,1)S(1)}, bf16[8,9216]{1,0:T(8,128)(2,1)S(1)}, u32[]{:S(2)}, u32[]{:S(2)}) collective-permute-start(bf16[8,9216]{1,0:T(8,128)(2,1)S(1)} %copy-done.2), channel_id=1, source_target_pairs={{3,0},{4,1},{5,2},{6,3},{7,4},{8,5},{9,6},{10,7},{11,8},{12,9},{13... | collective-permute-start | bytes 442376 | tf_op jit(solution)/shard_map/ppermute | solution.py:41
  52.4 1.3 copy-start
  56.1 2.4 %copy-start.7 = (f32[4096]{0:T(1024)S(1)}, f32[4096]{0:T(1024)}, u32[]{:S(2)}) copy-start(f32[4096]{0:T(1024)} %slice_bitcast_fusion.3) | copy-start | bytes 49156
  56.1 2.4 %copy-start.10 = (s32[4]{0:T(128)S(1)}, s32[4]{0:T(128)}, u32[]{:S(2)}) copy-start(s32[4]{0:T(128)} %get-tuple-element.38) | copy-start | bytes 52
  56.1 2.4 %copy-start.11 = (s32[4]{0:T(128)S(1)}, s32[4]{0:T(128)}, u32[]{:S(2)}) copy-start(s32[4]{0:T(128)} %get-tuple-element.39) | copy-start | bytes 52
  58.4 0.9 copy-start.14
  58.4 0.9 copy-start.16
  58.4 1.0 copy-start.4
  58.6 1.0 copy-start.3
  59.5 1.1 copy-start.1
  84.3 0.7 copy-start.9
  108.4 18.0 %copy-start.23 = (u32[256]{0:T(256)S(1)}, u32[256]{0:T(256)}, u32[]{:S(2)}) copy-start(u32[256]{0:T(256)} %constant.128) | copy-start | bytes 3076
  108.5 12.6 %collective-permute-start.6 = (bf16[8,1152]{1,0:T(8,128)(2,1)S(1)}, bf16[8,1152]{1,0:T(8,128)(2,1)S(1)}, u32[]{:S(2)}, u32[]{:S(2)}) collective-permute-start(bf16[8,1152]{1,0:T(8,128)(2,1)S(1)} %get-tuple-element.33), channel_id=1, source_target_pairs={{0,1},{1,2},{2,3},{3,4},{4,5},{5,6},{6,7},{7,8},{8,9},{9,10},{10,1... | collective-permute-start | bytes 55304 | tf_op jit(solution)/shard_map/ppermute | solution.py:41
  113.8 7.3 %collective-permute-start.7 = (bf16[8,1152]{1,0:T(8,128)(2,1)S(1)}, bf16[8,1152]{1,0:T(8,128)(2,1)S(1)}, u32[]{:S(2)}, u32[]{:S(2)}) collective-permute-start(bf16[8,1152]{1,0:T(8,128)(2,1)S(1)} %get-tuple-element.35), channel_id=1, source_target_pairs={{0,2},{1,3},{2,4},{3,5},{4,6},{5,7},{6,8},{7,9},{8,10},{9,11},{10,... | collective-permute-start | bytes 55304 | tf_op jit(solution)/shard_map/ppermute | solution.py:41
  115.1 6.8 %collective-permute-start.8 = (bf16[8,1152]{1,0:T(8,128)(2,1)S(1)}, bf16[8,1152]{1,0:T(8,128)(2,1)S(1)}, u32[]{:S(2)}, u32[]{:S(2)}) collective-permute-start(bf16[8,1152]{1,0:T(8,128)(2,1)S(1)} %get-tuple-element.34), channel_id=1, source_target_pairs={{0,3},{1,4},{2,5},{3,6},{4,7},{5,8},{6,9},{7,10},{8,11},{9,12},{10... | collective-permute-start | bytes 55304 | tf_op jit(solution)/shard_map/ppermute | solution.py:41
  122.7 6.7 %copy-start.22 = (u32[256]{0:T(256)S(1)}, u32[256]{0:T(256)}, u32[]{:S(2)}) copy-start(u32[256]{0:T(256)} %constant.133) | copy-start | bytes 3076
  122.7 15.3 %copy-start.21 = (u32[256]{0:T(256)S(1)}, u32[256]{0:T(256)}, u32[]{:S(2)}) copy-start(u32[256]{0:T(256)} %constant.138) | copy-start | bytes 3076
  122.7 26.0 %copy-start.20 = (u32[256]{0:T(256)S(1)}, u32[256]{0:T(256)}, u32[]{:S(2)}) copy-start(u32[256]{0:T(256)} %constant.143) | copy-start | bytes 3076
  122.7 32.5 %copy-start.19 = (u32[256]{0:T(256)S(1)}, u32[256]{0:T(256)}, u32[]{:S(2)}) copy-start(u32[256]{0:T(256)} %constant.148) | copy-start | bytes 3076
  122.7 59.9 %all-to-all-start.2 = ((f32[8,8,1152]{2,1,0:T(8,128)}), f32[8,8,1152]{2,1,0:T(8,128)S(1)}, u32[]{:S(2)}, u32[]{:S(2)}) async-start(f32[8,8,1152]{2,1,0:T(8,128)} %broadcast_in_dim.44), calls=%async_computation.2 | async-start | bytes 589824 | tf_op jit(solution)/shard_map/all_to_all | solution.py:24
